TPU v7x, 32 devices: a whole 2x2x4 slice. The times are simulated.
32 devices in a mesh: grp: 2 (over y), tm: 4 (over z), space: 4 (over x, core).
Axes of the slice: x: 2, y: 2, z: 4, core: 2. Of those that a mesh axis runs over, the one named last changes fastest.
Arguments:
- forcing: float32 [32, 32, 8, 128], P(('grp', 'tm'), 'space'), parts along dimension 0, may hold values from -6 to 6
- start_field: float32 [64, 8, 128], P(('grp', 'space')), parts along dimension 0, may hold values from -6 to 6
- velocity: float32 [3, 32, 8, 128], P(None, 'space'), may hold values from -0.5 to 0.5
- diffusivity: float32 [2], P('grp'), parts along dimension 0, may hold values from 0.3 to 1
Outputs:
- iterate: float32 [32, 32, 8, 128], P(('grp', 'tm'), 'space'), parts along dimension 0
There are 2 independent parts, one for each index of `grp`. A program takes and returns all parts, laid end to end along the dimension named above; an argument that names none is the same for every part. Nothing has to cross between parts.
All inputs are finite; a program needn't handle non-finite values.
Results may differ from a plain program's by a relative error of at most 0.0001.
Values sent between devices are 32-bit elements; how exact they have to be, the bound alone decides.
A program may use at most 64 MiB of HBM per device.

v0:
```python
import jax
import jax.numpy as jnp
from jax import lax
from jax.sharding import PartitionSpec as P

SWEEPS = 4


time_unit = 0.5


def passed_along(value, axis, steps):
    count = lax.axis_size(axis)
    leading, last = (max(0, -steps), min(count, count - steps))
    return lax.ppermute(value, axis, [(source, source + steps) for source in range(leading, last)])


def neighbour_sum(padded, velocity, kappa_value):
    middle = padded[1:-1]
    higher = padded[2:]
    beneath = padded[:-2]
    east_side = jnp.roll(middle, -1, axis=1)
    west_side = jnp.roll(middle, 1, axis=1)
    north_side = jnp.roll(middle, -1, axis=2)
    south_side = jnp.roll(middle, 1, axis=2)
    diffused = kappa_value * (higher + beneath + east_side + west_side + north_side + south_side)
    carried = (
        velocity[0] * (higher - beneath)
        + velocity[1] * (east_side - west_side)
        + velocity[2] * (north_side - south_side)
    )
    return diffused - 0.5 * carried


def local(forcing, start_field, velocity, diffusivity):
    kappa_value = diffusivity[0]
    time_count = lax.axis_size("tm")
    time_rank = lax.axis_index("tm")
    coarse_levels = (time_count.bit_length() - 1) // 2
    slab_rows = forcing.shape[1]
    forcing_used, start_used, velocity_all = (
        lax.all_gather(forcing, "space", axis=1, tiled=True),
        lax.all_gather(start_field, "space", axis=0, tiled=True),
        lax.all_gather(velocity, "space", axis=1, tiled=True),
    )

    def propagate(source, time_step):
        diagonal = 1.0 + 6.0 * time_step * kappa_value
        values = source
        for repeat in range(SWEEPS):
            padded = jnp.pad(values, ((1, 1), (0, 0), (0, 0)))
            values = (
                source + time_step * neighbour_sum(padded, velocity_all, kappa_value)
            ) / diagonal
        return values

    def advance(values, stride):
        return passed_along(values, "tm", stride)

    starting = (time_rank == 0).astype(jnp.float32)

    def relax_fine(iterate):
        previous = advance(iterate[3], 1) + starting * start_used
        first_point = propagate(previous, time_unit) + forcing_used[0]
        second_point = propagate(first_point, time_unit) + forcing_used[1]
        third_point = propagate(second_point, time_unit) + forcing_used[2]
        return jnp.stack([first_point, second_point, third_point, iterate[3]])

    def solve_coarse(level_index, right_side):
        stride = 4 ** (level_index - 1)
        time_step = time_unit * 4.0**level_index
        active = (time_rank + 1) % stride == 0
        position = (time_rank + 1) // stride

        def step_where(values, chosen):
            return jnp.where(
                chosen, propagate(advance(values, stride), time_step) + right_side, values
            )

        correction = jnp.zeros_like(right_side)
        if level_index == coarse_levels:
            for offset in range(1, 5):
                correction = step_where(correction, active & (position == offset))
            return jnp.where(active, correction, 0.0)

        def relax_points(values):
            for offset in range(1, 4):
                values = step_where(values, active & (position % 4 == offset))
            return values

        correction = relax_points(correction)
        residual = right_side + propagate(advance(correction, stride), time_step) - correction
        correction = correction + solve_coarse(level_index + 1, residual)
        correction = relax_points(correction)
        return jnp.where(active, correction, 0.0)

    iterate = jnp.zeros_like(forcing_used)
    iterate = relax_fine(iterate)
    coarse_point = propagate(iterate[2], time_unit) + forcing_used[3]
    iterate = jnp.concatenate([iterate[:3], coarse_point[None]], axis=0)
    iterate = relax_fine(iterate)
    residual = forcing_used[3] + propagate(iterate[2], time_unit) - iterate[3]
    correction = solve_coarse(1, residual)
    iterate = jnp.concatenate([iterate[:3], (iterate[3] + correction)[None]], axis=0)
    iterate = relax_fine(iterate)
    iterate = lax.dynamic_slice_in_dim(iterate, lax.axis_index("space") * slab_rows, slab_rows, 1)
    return iterate


def solution(mesh):
    placed = (
        P(("grp", "tm"), "space", None, None),
        P(("grp", "space"), None, None),
        P(None, "space", None, None),
        P("grp"),
    )
    return jax.shard_map(
        local,
        mesh=mesh,
        in_specs=placed,
        out_specs=P(("grp", "tm"), "space", None, None),
        check_vma=False,
    )
```

profile of v0, /device:TPU:16, one launch (start us, length us, event | category | flops | bytes accessed | tf_op | source)
XLA Modules:
  0.0 86.3 jit_solution(8612580520080403469)
XLA Ops:
  0.0 3.6 %collective-permute-start = (f32[32,8,128]{2,1,0:T(8,128)S(1)}, f32[32,8,128]{2,1,0:T(8,128)S(1)}, u32[]{:S(2)}, u32[]{:S(2)}) collective-permute-start(f32[32,8,128]{2,1,0:T(8,128)S(1)} %broadcast.131), channel_id=1, source_target_pairs={{0,4},{4,8},{8,12},{1,5},{5,9},{9,13},{2,6},{6,10},{10,14},{3,7},{... | collective-permute-start | bytes 393224 | tf_op jit(solution)/shard_map/ppermute | solution.py:15
  4.3 5.6 %all_gather.9 = f32[32,8,128]{2,1,0:T(8,128)S(1)} all-gather(f32[8,8,128]{2,1,0:T(8,128)} %param.5), channel_id=1, replica_groups=mesh['grp'=2,'tm'=4,'space'=4] {'space'}, dimensions={0}, use_global_device_ids=true | all-gather | bytes 163840 | tf_op jit(solution)/shard_map/all_gather | solution.py:43
  9.9 7.4 %all_gather.11 = f32[4,32,8,128]{3,2,1,0:T(8,128)S(1)} all-gather(f32[4,8,8,128]{3,2,1,0:T(8,128)S(1)} %copy-done), channel_id=1, replica_groups=mesh['grp'=2,'tm'=4,'space'=4] {'space'}, dimensions={1}, use_global_device_ids=true | all-gather | bytes 655360 | tf_op jit(solution)/shard_map/all_gather | solution.py:42
  17.3 6.6 %all_gather.10 = f32[3,32,8,128]{3,2,1,0:T(8,128)S(1)} all-gather(f32[3,8,8,128]{3,2,1,0:T(8,128)S(1)} %copy-done.1), channel_id=1, replica_groups=mesh['grp'=2,'tm'=4,'space'=4] {'space'}, dimensions={1}, use_global_device_ids=true | all-gather | bytes 491520 | tf_op jit(solution)/shard_map/all_gather | solution.py:44
  32.3 0.2 divide_add_fusion.5
  32.5 2.1 %collective-permute-start.1 = (f32[32,8,128]{2,1,0:T(8,128)S(1)}, f32[32,8,128]{2,1,0:T(8,128)S(1)}, u32[]{:S(2)}, u32[]{:S(2)}) collective-permute-start(f32[32,8,128]{2,1,0:T(8,128)S(1)} %divide_add_fusion.5), channel_id=1, source_target_pairs={{0,4},{4,8},{8,12},{1,5},{5,9},{9,13},{2,6},{6,10},{10,14},{3,7},{... | collective-permute-start | bytes 393224 | tf_op jit(solution)/shard_map/ppermute | solution.py:15
  34.7 5.5 %collective-permute-done.1 = f32[32,8,128]{2,1,0:T(8,128)S(1)} collective-permute-done((f32[32,8,128]{2,1,0:T(8,128)S(1)}, f32[32,8,128]{2,1,0:T(8,128)S(1)}, u32[]{:S(2)}, u32[]{:S(2)}) %collective-permute-start.1) | collective-permute-done | bytes 131104 | tf_op jit(solution)/shard_map/ppermute | solution.py:15
  41.8 0.2 divide_add_fusion.4
  43.6 0.2 divide_add_fusion.3
  45.3 0.2 divide_add_fusion.2
  45.8 0.2 add_divide_fusion.20
  47.1 0.4 add_select_fusion.2
  47.5 2.2 %collective-permute-start.2 = (f32[32,8,128]{2,1,0:T(8,128)S(1)}, f32[32,8,128]{2,1,0:T(8,128)S(1)}, u32[]{:S(2)}, u32[]{:S(2)}) collective-permute-start(f32[32,8,128]{2,1,0:T(8,128)S(1)} %get-tuple-element.5), channel_id=1, source_target_pairs={{0,4},{4,8},{8,12},{1,5},{5,9},{9,13},{2,6},{6,10},{10,14},{3,7},{... | collective-permute-start | bytes 393224 | tf_op jit(solution)/shard_map/ppermute | solution.py:15
  49.7 4.6 %collective-permute-done.2 = f32[32,8,128]{2,1,0:T(8,128)S(1)} collective-permute-done((f32[32,8,128]{2,1,0:T(8,128)S(1)}, f32[32,8,128]{2,1,0:T(8,128)S(1)}, u32[]{:S(2)}, u32[]{:S(2)}) %collective-permute-start.2) | collective-permute-done | bytes 131104 | tf_op jit(solution)/shard_map/ppermute | solution.py:15
  56.0 0.2 add_select_fusion.1
  56.2 2.4 %collective-permute-start.3 = (f32[32,8,128]{2,1,0:T(8,128)S(1)}, f32[32,8,128]{2,1,0:T(8,128)S(1)}, u32[]{:S(2)}, u32[]{:S(2)}) collective-permute-start(f32[32,8,128]{2,1,0:T(8,128)S(1)} %add_select_fusion.1), channel_id=1, source_target_pairs={{0,4},{4,8},{8,12},{1,5},{5,9},{9,13},{2,6},{6,10},{10,14},{3,7},{... | collective-permute-start | bytes 393224 | tf_op jit(solution)/shard_map/ppermute | solution.py:15
  58.6 4.4 %collective-permute-done.3 = f32[32,8,128]{2,1,0:T(8,128)S(1)} collective-permute-done((f32[32,8,128]{2,1,0:T(8,128)S(1)}, f32[32,8,128]{2,1,0:T(8,128)S(1)}, u32[]{:S(2)}, u32[]{:S(2)}) %collective-permute-start.3) | collective-permute-done | bytes 131104 | tf_op jit(solution)/shard_map/ppermute | solution.py:15
  64.6 0.2 add_select_fusion
  64.8 2.4 %collective-permute-start.4 = (f32[32,8,128]{2,1,0:T(8,128)S(1)}, f32[32,8,128]{2,1,0:T(8,128)S(1)}, u32[]{:S(2)}, u32[]{:S(2)}) collective-permute-start(f32[32,8,128]{2,1,0:T(8,128)S(1)} %add_select_fusion), channel_id=1, source_target_pairs={{0,4},{4,8},{8,12},{1,5},{5,9},{9,13},{2,6},{6,10},{10,14},{3,7},{... | collective-permute-start | bytes 393224 | tf_op jit(solution)/shard_map/ppermute | solution.py:15
  67.2 4.4 %collective-permute-done.4 = f32[32,8,128]{2,1,0:T(8,128)S(1)} collective-permute-done((f32[32,8,128]{2,1,0:T(8,128)S(1)}, f32[32,8,128]{2,1,0:T(8,128)S(1)}, u32[]{:S(2)}, u32[]{:S(2)}) %collective-permute-start.4) | collective-permute-done | bytes 131104 | tf_op jit(solution)/shard_map/ppermute | solution.py:15
  73.2 0.2 select_add_fusion
  73.4 2.6 %collective-permute-start.5 = (f32[32,8,128]{2,1,0:T(8,128)S(1)}, f32[32,8,128]{2,1,0:T(8,128)S(1)}, u32[]{:S(2)}, u32[]{:S(2)}) collective-permute-start(f32[32,8,128]{2,1,0:T(8,128)S(1)} %select_add_fusion), channel_id=1, source_target_pairs={{0,4},{4,8},{8,12},{1,5},{5,9},{9,13},{2,6},{6,10},{10,14},{3,7},{... | collective-permute-start | bytes 393224 | tf_op jit(solution)/shard_map/ppermute | solution.py:15
  76.1 4.2 %collective-permute-done.5 = f32[32,8,128]{2,1,0:T(8,128)S(1)} collective-permute-done((f32[32,8,128]{2,1,0:T(8,128)S(1)}, f32[32,8,128]{2,1,0:T(8,128)S(1)}, u32[]{:S(2)}, u32[]{:S(2)}) %collective-permute-start.5) | collective-permute-done | bytes 131104 | tf_op jit(solution)/shard_map/ppermute | solution.py:15
  85.6 0.7 fusion.2
  (298 shorter events, 22.6 us)
Async XLA Ops:
  0.0 9.9 %copy-start = (f32[4,8,8,128]{3,2,1,0:T(8,128)S(1)}, f32[4,8,8,128]{3,2,1,0:T(8,128)}, u32[]{:S(2)}) copy-start(f32[4,8,8,128]{3,2,1,0:T(8,128)} %param.4) | copy-start | bytes 393220
  0.0 23.9 %collective-permute-start = (f32[32,8,128]{2,1,0:T(8,128)S(1)}, f32[32,8,128]{2,1,0:T(8,128)S(1)}, u32[]{:S(2)}, u32[]{:S(2)}) collective-permute-start(f32[32,8,128]{2,1,0:T(8,128)S(1)} %broadcast.131), channel_id=1, source_target_pairs={{0,4},{4,8},{8,12},{1,5},{5,9},{9,13},{2,6},{6,10},{10,14},{3,7},{... | collective-permute-start | bytes 393224 | tf_op jit(solution)/shard_map/ppermute | solution.py:15
  9.9 7.4 %copy-start.1 = (f32[3,8,8,128]{3,2,1,0:T(8,128)S(1)}, f32[3,8,8,128]{3,2,1,0:T(8,128)}, u32[]{:S(2)}) copy-start(f32[3,8,8,128]{3,2,1,0:T(8,128)} %param.6) | copy-start | bytes 294916
  32.5 7.6 %collective-permute-start.1 = (f32[32,8,128]{2,1,0:T(8,128)S(1)}, f32[32,8,128]{2,1,0:T(8,128)S(1)}, u32[]{:S(2)}, u32[]{:S(2)}) collective-permute-start(f32[32,8,128]{2,1,0:T(8,128)S(1)} %divide_add_fusion.5), channel_id=1, source_target_pairs={{0,4},{4,8},{8,12},{1,5},{5,9},{9,13},{2,6},{6,10},{10,14},{3,7},{... | collective-permute-start | bytes 393224 | tf_op jit(solution)/shard_map/ppermute | solution.py:15
  47.5 6.9 %collective-permute-start.2 = (f32[32,8,128]{2,1,0:T(8,128)S(1)}, f32[32,8,128]{2,1,0:T(8,128)S(1)}, u32[]{:S(2)}, u32[]{:S(2)}) collective-permute-start(f32[32,8,128]{2,1,0:T(8,128)S(1)} %get-tuple-element.5), channel_id=1, source_target_pairs={{0,4},{4,8},{8,12},{1,5},{5,9},{9,13},{2,6},{6,10},{10,14},{3,7},{... | collective-permute-start | bytes 393224 | tf_op jit(solution)/shard_map/ppermute | solution.py:15
  56.2 6.9 %collective-permute-start.3 = (f32[32,8,128]{2,1,0:T(8,128)S(1)}, f32[32,8,128]{2,1,0:T(8,128)S(1)}, u32[]{:S(2)}, u32[]{:S(2)}) collective-permute-start(f32[32,8,128]{2,1,0:T(8,128)S(1)} %add_select_fusion.1), channel_id=1, source_target_pairs={{0,4},{4,8},{8,12},{1,5},{5,9},{9,13},{2,6},{6,10},{10,14},{3,7},{... | collective-permute-start | bytes 393224 | tf_op jit(solution)/shard_map/ppermute | solution.py:15
  64.8 6.9 %collective-permute-start.4 = (f32[32,8,128]{2,1,0:T(8,128)S(1)}, f32[32,8,128]{2,1,0:T(8,128)S(1)}, u32[]{:S(2)}, u32[]{:S(2)}) collective-permute-start(f32[32,8,128]{2,1,0:T(8,128)S(1)} %add_select_fusion), channel_id=1, source_target_pairs={{0,4},{4,8},{8,12},{1,5},{5,9},{9,13},{2,6},{6,10},{10,14},{3,7},{... | collective-permute-start | bytes 393224 | tf_op jit(solution)/shard_map/ppermute | solution.py:15
  73.4 6.9 %collective-permute-start.5 = (f32[32,8,128]{2,1,0:T(8,128)S(1)}, f32[32,8,128]{2,1,0:T(8,128)S(1)}, u32[]{:S(2)}, u32[]{:S(2)}) collective-permute-start(f32[32,8,128]{2,1,0:T(8,128)S(1)} %select_add_fusion), channel_id=1, source_target_pairs={{0,4},{4,8},{8,12},{1,5},{5,9},{9,13},{2,6},{6,10},{10,14},{3,7},{... | collective-permute-start | bytes 393224 | tf_op jit(solution)/shard_map/ppermute | solution.py:15
where the time goes:
time: 87.2 us; the launch traced here: 86.3 us
  waiting for transfers between devices  23.3 us (27%)
  blocking collectives  19.6 us (22%)
  starting transfers between devices  15.4 us (18%)
  local copies, waits for them, and re-layouts  13.8 us (16%)
  other arithmetic  11.4 us (13%)
  between operations  2.92 us (3%)
    ppermute x6, waiting for transfers between devices, passed_along(): lax.ppermute(value, axis, [(source, source + steps) for source in range(l...  23.3 us
    ppermute x6, starting transfers between devices, passed_along(): lax.ppermute(value, axis, [(source, source + steps) for source in range(l...  15.4 us
    slice x120, local copies, waits for them, and re-layouts, neighbour_sum(): north_side = jnp.roll(middle, -1, axis=2)  11.2 us
    div x45, other arithmetic, propagate(): (source + time_step * neighbour_sum(padded, velocity_all, kappa_value)) /...  7.89 us
    all_gather x1, blocking collectives, local(): lax.all_gather(forcing, 'space', axis=1, tiled=True)  7.39 us
    all_gather x1, blocking collectives, local(): lax.all_gather(velocity, 'space', axis=1, tiled=True)  6.55 us
    all_gather x1, blocking collectives, local(): lax.all_gather(start_field, 'space', axis=0, tiled=True)  5.63 us
    slice x120, local copies, waits for them, and re-layouts, neighbour_sum(): east_side = jnp.roll(middle, -1, axis=1)  2.62 us
  transfers between devices with their start and end apart: 6, of which 5 were waited for; matrix products, arithmetic and copies ran while one was open for 0% of the time, Pallas kernels for 0%

commit v1 on v0

--- a/solution.py
+++ b/solution.py
@@ -1,10 +1,14 @@
+import functools
+
 import jax
 import jax.numpy as jnp
 from jax import lax
+from jax.experimental import pallas as pl
+from jax.experimental.pallas import tpu as pltpu
 from jax.sharding import PartitionSpec as P
 
 SWEEPS = 4
-
+BLOCK = 4
 
 time_unit = 0.5
 
@@ -32,7 +36,7 @@
     return diffused - 0.5 * carried
 
 
-def local(forcing, start_field, velocity, diffusivity):
+def deep_local(forcing, start_field, velocity, diffusivity):
     kappa_value = diffusivity[0]
     time_count = lax.axis_size("tm")
     time_rank = lax.axis_index("tm")
@@ -107,6 +111,259 @@
     return iterate
 
 
+def kernel(
+    spaces, times,
+    f_ref, u_ref, v_ref, k_ref, out_ref,
+    fields, vel, tab, scaled, ping, pong, chain, got, echo, err,
+    local_sem, near_send, near_recv, far_send, far_recv, pass_send, pass_recv,
+    hop_send, hop_recv, swap_send, swap_recv,
+):
+    slab = f_ref.shape[1]
+    depth = vel.shape[1]
+    s = lax.axis_index("space")
+    t = lax.axis_index("tm")
+    mate = s + 1 - 2 * lax.rem(s, 2)
+    base = pl.multiple_of(s * slab, slab)
+    pairs = spaces // 2
+    kappa = k_ref[0]
+
+    own = pl.ds(base, slab)
+    pieces = [vel.at[:, own]] + [fields.at[i, own] for i in range(BLOCK + 1)]
+    sources = [v_ref, u_ref] + [f_ref.at[i] for i in range(BLOCK)]
+    locals_ = [
+        pltpu.make_async_copy(a, b, local_sem.at[i])
+        for i, (a, b) in enumerate(zip(sources, pieces))
+    ]
+    for copy in locals_:
+        copy.start()
+
+    barrier = pltpu.get_barrier_semaphore()
+    for k in range(1, spaces):
+        pl.semaphore_signal(
+            barrier, inc=1, device_id={"space": lax.rem(s + k, spaces)},
+            device_id_type=pl.DeviceIdType.MESH)
+    for k in range(1, times):
+        pl.semaphore_signal(
+            barrier, inc=1, device_id={"tm": lax.rem(t + k, times)},
+            device_id_type=pl.DeviceIdType.MESH)
+    pl.semaphore_wait(barrier, spaces - 1 + times - 1)
+
+    def piece(i, owner):
+        rows = pl.ds(pl.multiple_of(owner * slab, slab), slab)
+        return vel.at[:, rows] if i == 0 else fields.at[i - 1, rows]
+
+    def far_copy(i, k):
+        return pltpu.make_async_remote_copy(
+            piece(i, s), piece(i, s), far_send.at[k - 1, i], far_recv.at[k - 1, i],
+            device_id={"space": lax.rem(s + 2 * k, spaces)},
+            device_id_type=pl.DeviceIdType.MESH)
+
+    def near_copy(i):
+        return pltpu.make_async_remote_copy(
+            piece(i, s), piece(i, s), near_send.at[i], near_recv.at[i],
+            device_id={"space": mate}, device_id_type=pl.DeviceIdType.MESH)
+
+    def origin(k):
+        return lax.rem(s - 2 * k + spaces, spaces)
+
+    def pass_copy(i, k):
+        return pltpu.make_async_remote_copy(
+            piece(i, origin(k)), piece(i, origin(k)), pass_send.at[k - 1, i], pass_recv.at[k - 1, i],
+            device_id={"space": mate}, device_id_type=pl.DeviceIdType.MESH)
+
+    def far_arrived(i, k):
+        return pltpu.make_async_copy(piece(i, origin(k)), piece(i, origin(k)), far_recv.at[k - 1, i])
+
+    total = BLOCK + 2
+    order = [0, 1, 2, 3, 4, 5]
+    for i in order:
+        locals_[i].wait()
+        for k in range(1, pairs):
+            far_copy(i, k).start()
+        near_copy(i).start()
+
+    def collect(i):
+        for k in range(1, pairs):
+            far_copy(i, k).wait_recv()
+            pass_copy(i, k).start()
+        near_copy(i).wait_recv()
+        for k in range(1, pairs):
+            pass_copy(i, k).wait_recv()
+
+    steps = (time_unit, time_unit * 4.0)
+    inverse = []
+    for h in steps:
+        inverse.append(1.0 / jnp.full((8, 128), 1.0 + 6.0 * h * kappa, jnp.float32))
+
+    def make_tables(level):
+        h = steps[level]
+
+        def plane(z, carry):
+            for d in range(3):
+                half = 0.5 * vel[d, z]
+                tab[level, 2 * d, z] = (h * inverse[level]) * (kappa - half)
+                tab[level, 2 * d + 1, z] = (h * inverse[level]) * (kappa + half)
+            return carry
+
+        lax.fori_loop(0, depth, plane, 0)
+
+    def phi(level, load, store):
+        put0 = lambda z, v: ping.__setitem__(z, v)
+        stages = [
+            (load, lambda z, v: ping.__setitem__(z, v)),
+            (lambda z: ping[z], lambda z, v: pong.__setitem__(z, v)),
+            (lambda z: pong[z], lambda z, v: ping.__setitem__(z, v)),
+            (lambda z: ping[z], store),
+        ]
+        for number, (read, write) in enumerate(stages):
+            below, here = None, read(0)
+            for z in range(depth):
+                above = read(z + 1) if z + 1 < depth else None
+                if number == 0:
+                    value = here * inverse[level]
+                    scaled[z] = value
+                else:
+                    value = scaled[z]
+                x = tab[level, 2, z] * pltpu.roll(here, 7, 0) + tab[level, 3, z] * pltpu.roll(here, 1, 0)
+                y = tab[level, 4, z] * pltpu.roll(here, 127, 1) + tab[level, 5, z] * pltpu.roll(here, 1, 1)
+                if above is not None:
+                    value = value + tab[level, 0, z] * above
+                if below is not None:
+                    value = value + tab[level, 1, z] * below
+                value = value + (x + y)
+                write(z, value)
+                below, here = here, above
+
+    collect(0)
+    make_tables(0)
+
+    collect(1)
+    collect(2)
+
+    @pl.when(t == 0)
+    def _():
+        phi(0, lambda z: fields[0, z],
+            lambda z, v: chain.__setitem__((0, z), v + fields[1, z]))
+
+    @pl.when(t > 0)
+    def _():
+        chain[0] = fields[1]
+
+    for i in range(1, BLOCK):
+        collect(i + 2)
+        if i < BLOCK:
+            pass
+
+    def advance(i, carry):
+        phi(0, lambda z: chain[i - 1, z],
+            lambda z, v: chain.__setitem__((i, z), v + fields[i + 1, z]))
+        return carry
+
+    lax.fori_loop(1, BLOCK, advance, 0)
+
+    half = depth // 2
+    rows = pl.ds(pl.multiple_of(lax.rem(s, 2) * half, half), half)
+
+    def hop_copy(k):
+        return pltpu.make_async_remote_copy(
+            chain.at[BLOCK - 1, rows], got.at[t, rows], hop_send.at[k - 1], hop_recv.at[t],
+            device_id={"tm": lax.rem(t + k, times)}, device_id_type=pl.DeviceIdType.MESH)
+
+    for k in range(times - 1, 0, -1):
+        @pl.when(t + k < times)
+        def _():
+            hop_copy(k).start()
+
+    make_tables(1)
+
+    def swap_copy(j):
+        return pltpu.make_async_remote_copy(
+            got.at[j, rows], got.at[j, rows], swap_send.at[j], swap_recv.at[j],
+            device_id={"space": mate}, device_id_type=pl.DeviceIdType.MESH)
+
+    def hop_arrival(j):
+        return pltpu.make_async_remote_copy(
+            chain.at[BLOCK - 1, rows], got.at[j, rows], hop_send.at[0], hop_recv.at[j],
+            device_id={"tm": lax.rem(t + 1, times)}, device_id_type=pl.DeviceIdType.MESH)
+
+    for j in range(times - 2, -1, -1):
+        @pl.when(t > j)
+        def _():
+            hop_arrival(j).wait_recv()
+            swap_copy(j).start()
+            swap_copy(j).wait_recv()
+            echo[j] = got[j]
+
+            def again(i, carry):
+                phi(0, lambda z: echo[j, z], lambda z, v: echo.__setitem__((j, z), v))
+                return carry
+
+            lax.fori_loop(0, BLOCK, again, 0)
+
+    @pl.when(t == 0)
+    def _():
+        for i in range(BLOCK):
+            out_ref[i] = chain[i, own]
+
+    @pl.when(t > 0)
+    def _():
+        err[0] = jnp.zeros(err.shape[1:], jnp.float32)
+        err[1] = echo[0]
+
+        def correct(m, carry):
+            phi(1, lambda z: err[m - 1, z],
+                lambda z, v: err.__setitem__((m, z), v + echo[m - 1, z]))
+            return carry
+
+        lax.fori_loop(2, t + 1, correct, 0)
+        echo[0] = got[t - 1] + err[t - 1]
+
+        def relax(i, carry):
+            phi(0, lambda z: echo[0, z], lambda z, v: echo.__setitem__((0, z), v))
+            out_ref[i] = chain[i, own] + echo[0, own]
+            return carry
+
+        lax.fori_loop(0, BLOCK - 1, relax, 0)
+        out_ref[BLOCK - 1] = chain[BLOCK - 1, own] + err[t, own]
+
+    for i in range(total):
+        near_copy(i).wait_send()
+        for k in range(1, pairs):
+            far_copy(i, k).wait_send()
+            pass_copy(i, k).wait_send()
+    for k in range(1, times):
+        @pl.when(t + k < times)
+        def _():
+            hop_copy(k).wait_send()
+    for j in range(times - 1):
+        @pl.when(t > j)
+        def _():
+            swap_copy(j).wait_send()
+
+
+def shallow_local(forcing, start_field, velocity, diffusivity):
+    spaces, times = lax.axis_size("space"), lax.axis_size("tm")
+    slab = forcing.shape[1]
+    field = (spaces * slab,) + forcing.shape[2:]
+    dma = pltpu.SemaphoreType.DMA
+    vmem = lambda *shape: pltpu.VMEM(shape + field, jnp.float32)
+    pieces, pairs = BLOCK + 2, max(spaces // 2 - 1, 1)
+    return pl.pallas_call(
+        functools.partial(kernel, spaces, times),
+        out_shape=jax.ShapeDtypeStruct(forcing.shape, forcing.dtype),
+        in_specs=[pl.BlockSpec(memory_space=pl.ANY)] * 3 + [pl.BlockSpec(memory_space=pltpu.SMEM)],
+        out_specs=pl.BlockSpec(memory_space=pltpu.VMEM),
+        scratch_shapes=[
+            vmem(BLOCK + 1), vmem(3), vmem(2, 6), vmem(), vmem(), vmem(),
+            vmem(BLOCK), vmem(times), vmem(times), vmem(times + 1),
+            dma((pieces,)), dma((pieces,)), dma((pieces,)),
+            dma((pairs, pieces)), dma((pairs, pieces)), dma((pairs, pieces)), dma((pairs, pieces)),
+            dma((times,)), dma((times,)), dma((times,)), dma((times,)),
+        ],
+        compiler_params=pltpu.CompilerParams(collective_id=0, has_side_effects=True),
+    )(forcing, start_field, velocity, diffusivity)
+
+
 def solution(mesh):
     placed = (
         P(("grp", "tm"), "space", None, None),
@@ -114,8 +371,9 @@
         P(None, "space", None, None),
         P("grp"),
     )
+    one_level = mesh.shape["tm"] == BLOCK and mesh.shape["space"] % 2 == 0
     return jax.shard_map(
-        local,
+        shallow_local if one_level else deep_local,
         mesh=mesh,
         in_specs=placed,
         out_specs=P(("grp", "tm"), "space", None, None),

time: 87.2 us -> 31.5 us (0.36)
  Pallas kernels: 0 us -> 29.1 us
  waiting for transfers between devices: 23.3 us -> 0 us
  blocking collectives: 19.6 us -> 0 us
  starting transfers between devices: 15.4 us -> 0 us
  local copies, waits for them, and re-layouts: 13.8 us -> 1.57 us
  other arithmetic: 11.4 us -> 0 us
  between operations: 2.92 us -> 0.66 us
    pallas_call x0 -> x1, Pallas kernels: none -> 29.1 us  [shallow_local(): pl.pallas_call(functools.partial(kernel, spaces, times), out_shape=jax.Sh...]
    ppermute x6 -> x0, waiting for transfers between devices: 23.3 us -> none  [passed_along(): lax.ppermute(value, axis, [(source, source + steps) for source in range(l...]
    all_gather x3 -> x0, blocking collectives: 19.6 us -> none  [the longest x1 7.39 us: local(): lax.all_gather(forcing, 'space', axis=1, tiled=True)]
    ppermute x6 -> x0, starting transfers between devices: 15.4 us -> none  [passed_along(): lax.ppermute(value, axis, [(source, source + steps) for source in range(l...]
    slice x240 -> x0, local copies, waits for them, and re-layouts: 13.8 us -> none  [the longest x120 11.2 us: neighbour_sum(): north_side = jnp.roll(middle, -1, axis=2)]
    div x45 -> x0, other arithmetic: 7.89 us -> none  [propagate(): (source + time_step * neighbour_sum(padded, velocity_all, kappa_value)) /...]
    add x12 -> x0, other arithmetic: 1.86 us -> none  [the longest x3 0.54 us: relax_fine(): second_point = propagate(first_point, time_unit) + forcing_used[1]]
    unnamed x4 -> x1, local copies, waits for them, and re-layouts: 0.01 us -> 1.57 us
  transfers between devices with their start and end apart: 6 -> 0, of which waited for: 5 -> 0; matrix products, arithmetic and copies ran while one was open for 0% -> 0% of each run, Pallas kernels for 0% -> 0%
where the time goes in v1:
time: 31.5 us; the launch traced here: 31.3 us
  Pallas kernels  29.1 us (92%)
  local copies, waits for them, and re-layouts  1.57 us (5%)
  between operations  0.66 us (2%)
    pallas_call x1, Pallas kernels, shallow_local(): pl.pallas_call(functools.partial(kernel, spaces, times), out_shape=jax.Sh...  29.1 us
    unnamed x1, local copies, waits for them, and re-layouts  1.57 us

profile of v1, /device:TPU:16, one launch (start us, length us, event | category | flops | bytes accessed | tf_op | source)
XLA Modules:
  0.0 31.3 jit_solution(7834837238468505498)
XLA Ops:
  0.7 29.1 %shard_map.46 = f32[4,8,8,128]{3,2,1,0:T(8,128)} custom-call(f32[4,8,8,128]{3,2,1,0:T(8,128)} %f_ref.1, f32[8,8,128]{2,1,0:T(8,128)} %u_ref.1, f32[3,8,8,128]{3,2,1,0:T(8,128)} %v_ref.1, f32[1]{0:T(128)S(6)} %copy.6.k_ref), custom_call_target="tpu_custom_call" | custom-call | tf_op jit(solution)/shard_map/pallas_call | solution.py:351
  29.7 1.6 %copy.7 = f32[4,8,8,128]{3,2,1,0:T(8,128)} copy(f32[4,8,8,128]{3,2,1,0:T(8,128)} %shard_map.46) | data formatting | bytes 262144

commit v2 on v0

--- a/solution.py
+++ b/solution.py
@@ -1,10 +1,14 @@
+import functools
+
 import jax
 import jax.numpy as jnp
 from jax import lax
+from jax.experimental import pallas as pl
+from jax.experimental.pallas import tpu as pltpu
 from jax.sharding import PartitionSpec as P
 
 SWEEPS = 4
-
+BLOCK = 4
 
 time_unit = 0.5
 
@@ -32,7 +36,7 @@
     return diffused - 0.5 * carried
 
 
-def local(forcing, start_field, velocity, diffusivity):
+def deep_local(forcing, start_field, velocity, diffusivity):
     kappa_value = diffusivity[0]
     time_count = lax.axis_size("tm")
     time_rank = lax.axis_index("tm")
@@ -107,6 +111,347 @@
     return iterate
 
 
+def kernel(
+    spaces, times,
+    f_ref, u_ref, v_ref, k_ref, out_ref,
+    slabs, tab, scaled, ping, pong, chain, got, echo, prev, err,
+    local_sem, near_send, near_recv, far_send, far_recv, pass_send, pass_recv,
+    hop_send, hop_recv, swap_send, swap_recv, ready,
+):
+    MESH = pl.DeviceIdType.MESH
+    slab = f_ref.shape[1]
+    depth = spaces * slab
+    pad = (tab.shape[2] - depth) // 2
+    s = lax.axis_index("space")
+    t = lax.axis_index("tm")
+    mate = s + 1 - 2 * lax.rem(s, 2)
+    pairs = spaces // 2
+    kappa = k_ref[0]
+    own = pl.ds(pl.multiple_of(s * slab, slab), slab)
+    start, force = 3, 4
+
+    pieces = [(0, force), (force, force + 2), (force + 2, force + 3), (force + 3, force + 4)]
+    locals_ = [
+        pltpu.make_async_copy(v_ref, slabs.at[s, pl.ds(0, 3)], local_sem.at[0]),
+        pltpu.make_async_copy(u_ref, slabs.at[s, start], local_sem.at[1]),
+        pltpu.make_async_copy(f_ref, slabs.at[s, pl.ds(force, BLOCK)], local_sem.at[2]),
+    ]
+    for copy in locals_:
+        copy.start()
+
+    barrier = pltpu.get_barrier_semaphore()
+    for k in range(1, spaces):
+        pl.semaphore_signal(
+            barrier, inc=1, device_id={"space": lax.rem(s + k, spaces)}, device_id_type=MESH)
+
+    @pl.when(t > 0)
+    def _():
+        pl.semaphore_signal(barrier, inc=1, device_id={"tm": t - 1}, device_id_type=MESH)
+
+    @pl.when(t < times - 1)
+    def _():
+        pl.semaphore_signal(barrier, inc=1, device_id={"tm": t + 1}, device_id_type=MESH)
+
+    zero = jnp.zeros((8, 128), jnp.float32)
+    for z in list(range(pad)) + list(range(pad + depth, depth + 2 * pad)):
+        for level in range(2):
+            for c in range(6):
+                tab[level, c, z] = zero
+        for i in range(BLOCK):
+            chain[i, z] = zero
+        prev[z] = zero
+        err[0, z] = zero
+        err[1, z] = zero
+
+    def ends(low, high):
+        return jnp.where(t > 0, low, 0) + jnp.where(t < times - 1, high, 0)
+
+    pl.semaphore_wait(barrier, spaces - 1 + ends(1, 1))
+
+    def piece(i, owner):
+        low, high = pieces[i]
+        return slabs.at[owner, pl.ds(low, high - low)]
+
+    def origin(k, of=None):
+        return lax.rem((s if of is None else of) - 2 * k + spaces, spaces)
+
+    def remote(src, send, recv, **target):
+        return pltpu.make_async_remote_copy(
+            src, src, send, recv, device_id=target, device_id_type=MESH)
+
+    def far_copy(i, k):
+        return remote(piece(i, s), far_send.at[k - 1, i], far_recv.at[k - 1, i],
+                      space=lax.rem(s + 2 * k, spaces))
+
+    def near_copy(i):
+        return remote(piece(i, s), near_send.at[i], near_recv.at[i], space=mate)
+
+    def pass_copy(i, k):
+        return remote(piece(i, origin(k)), pass_send.at[k - 1, i], pass_recv.at[k - 1, i],
+                      space=mate)
+
+    for i in range(len(pieces)):
+        for copy in {0: locals_[:2], 1: locals_[2:]}.get(i, []):
+            copy.wait()
+        for k in range(1, pairs):
+            far_copy(i, k).start()
+        near_copy(i).start()
+
+    steps = (time_unit, time_unit * 4.0)
+    inverse = [1.0 / jnp.full((8, 128), 1.0 + 6.0 * h * kappa, jnp.float32) for h in steps]
+
+    def make_tables(owner):
+        scale = steps[0] * inverse[0]
+        middle, side = scale * kappa, scale * 0.5
+        first = pad + owner * slab
+        for z in range(slab):
+            for d in range(3):
+                part = side * slabs[owner, d, z]
+                tab[0, 2 * d, first + z] = middle - part
+                tab[0, 2 * d + 1, first + z] = middle + part
+
+    make_tables(s)
+    near_copy(0).wait_recv()
+    make_tables(mate)
+
+    for k in range(2, times):
+        @pl.when((t > 0) & (t - 1 + k < times))
+        def _():
+            pl.semaphore_signal(ready.at[k], inc=1, device_id={"tm": t - 1}, device_id_type=MESH)
+
+        @pl.when(t + k < times)
+        def _():
+            pl.semaphore_wait(ready.at[k], 1)
+
+    def forward(i):
+        for k in range(1, pairs):
+            far_copy(i, k).wait_recv()
+            pass_copy(i, k).start()
+
+    def settle(i):
+        near_copy(i).wait_recv()
+        for k in range(1, pairs):
+            pass_copy(i, k).wait_recv()
+
+    for k in range(1, pairs):
+        far_copy(0, k).wait_recv()
+        pass_copy(0, k).start()
+        make_tables(origin(k))
+    for k in range(1, pairs):
+        pass_copy(0, k).wait_recv()
+        make_tables(origin(k, mate))
+
+    def sweep(level, planes, read, base, write, tables):
+        low, high = planes
+        below = read(low - 1)
+        here = read(low)
+        for z in range(low, high):
+            above = read(z + 1)
+            weight = lambda c: tables[level, c, z]
+            x = weight(2) * pltpu.roll(here, 7, 0) + weight(3) * pltpu.roll(here, 1, 0)
+            y = weight(4) * pltpu.roll(here, 127, 1) + weight(5) * pltpu.roll(here, 1, 1)
+            value = base(z, here)
+            if above is not None:
+                value = value + weight(0) * above
+            if below is not None:
+                value = value + weight(1) * below
+            write(z, value + (x + y))
+            below, here = here, above
+
+    def phi(level, load, store, tables=None, scale=None, buffers=None, reach=None, last=None):
+        if reach is None:
+            full = (0, depth)
+            tables, scale, buffers = tab.at[:, :, pl.ds(pad, depth)], scaled, (ping, pong)
+            span = lambda sweeps: full
+            inside = lambda read: (lambda z: read(z) if 0 <= z < depth else None)
+        else:
+            span = lambda left: (pad - left - reach, pad + slab + left + reach)
+            inside = lambda read: read
+        one, two = buffers
+
+        def first(z, v):
+            value = v * inverse[level]
+            scale[z] = value
+            return value
+
+        put = lambda ref: (lambda z, v: ref.__setitem__(z, v))
+        get = lambda ref: inside(lambda z: ref[z])
+        later = lambda z, v: scale[z]
+        reads = [inside(load), get(one), get(two), get(one)]
+        writes = [put(one), put(two), put(one), store]
+        for n in range(SWEEPS):
+            if n == SWEEPS - 1 and last is not None:
+                last()
+            sweep(level, span(SWEEPS - 1 - n), reads[n],
+                  first if n == 0 else later, writes[n], tables)
+
+    def given(c, z):
+        return slabs[z // slab, c, z % slab]
+
+    def to_chain(i):
+        return lambda z, v: chain.__setitem__((i, pad + z), v + given(force + i, z))
+
+    @pl.when(t == 0)
+    def _():
+        phi(0, lambda z: given(start, z), lambda z, v: chain.__setitem__((0, pad + z), v))
+
+    forward(1)
+
+    @pl.when(t > 0)
+    def _():
+        settle(1)
+        for z in range(depth):
+            chain[0, pad + z] = given(force, z)
+
+    @pl.when(t == 0)
+    def _():
+        settle(1)
+        for z in range(depth):
+            chain[0, pad + z] = chain[0, pad + z] + given(force, z)
+
+    phi(0, lambda z: chain[0, pad + z], to_chain(1), last=lambda: forward(2))
+
+    def middle_of():
+        forward(3)
+        settle(2)
+
+    phi(0, lambda z: chain[1, pad + z], to_chain(2), last=middle_of)
+    phi(0, lambda z: chain[2, pad + z], to_chain(3), last=lambda: settle(3))
+
+    half = depth // 2
+    low = lax.rem(s, 2) * half
+    rows, chain_rows = pl.ds(low, half), pl.ds(pad + low, half)
+
+    def hop_copy(k, source=None):
+        return pltpu.make_async_remote_copy(
+            chain.at[BLOCK - 1, chain_rows], got.at[t if source is None else source, rows],
+            hop_send.at[k - 1], hop_recv.at[t if source is None else source],
+            device_id={"tm": lax.rem(t + k, times)}, device_id_type=MESH)
+
+    for k in range(times - 1, 0, -1):
+        @pl.when(t + k < times)
+        def _():
+            hop_copy(k).start()
+
+    ratio = (steps[1] * inverse[1]) / (steps[0] * inverse[0])
+
+    def coarse_tables(z, carry):
+        for c in range(6):
+            tab[1, c, pad + z] = ratio * tab[0, c, pad + z]
+        return carry
+
+    lax.fori_loop(0, depth, coarse_tables, 0)
+
+    def swap_copy(j):
+        return remote(got.at[j, rows], swap_send.at[j], swap_recv.at[j], space=mate)
+
+    chain_own = pl.ds(pad + s * slab, slab)
+
+    for j in range(times - 2, -1, -1):
+        @pl.when(t > j)
+        def _():
+            hop_copy(1, j).wait_recv()
+            swap_copy(j).start()
+            swap_copy(j).wait_recv()
+
+            def again(i, carry):
+                source = echo.at[j]
+                phi(0, lambda z: source[z], lambda z, v: source.__setitem__(z, v))
+                if j == 0:
+                    @pl.when(t == 1)
+                    def _():
+                        out_ref[i] = chain[i, chain_own] + echo[0, own]
+                return carry
+
+            echo[j] = got[j]
+            lax.fori_loop(0, BLOCK, again, 0)
+
+    @pl.when(t == 0)
+    def _():
+        for i in range(BLOCK):
+            out_ref[i] = chain[i, chain_own]
+
+    @pl.when(t > 1)
+    def _():
+        for z in range(depth):
+            err[1, pad + z] = echo[0, z]
+
+        def correct(m, carry):
+            phi(1, lambda z: err[1, pad + z],
+                lambda z, v: err.__setitem__((1, pad + z), v + echo[m - 1, z]))
+            return carry
+
+        lax.fori_loop(2, t, correct, 0)
+        for z in range(depth):
+            prev[pad + z] = got[t - 1, z] + err[1, pad + z]
+
+        window = pl.ds(s * slab, slab + 2 * pad)
+        near = dict(tables=tab.at[:, :, window], scale=scaled, buffers=(ping, pong))
+        points = prev.at[window]
+        errors = err.at[1, window]
+        added = [chain.at[i, window] for i in range(BLOCK)]
+        for i in range(BLOCK - 1):
+            reach = (BLOCK - 2 - i) * SWEEPS
+
+            def store(z, v):
+                value = v + added[i][z]
+                if pad <= z < pad + slab:
+                    out_ref[i, z - pad] = value
+                if reach:
+                    points[z] = v
+
+            phi(0, lambda z: points[z], store, reach=reach, **near)
+        gained = echo.at[t - 1, own]
+
+        def finish(z, v):
+            out_ref[BLOCK - 1, z - pad] = v + gained[z - pad] + added[BLOCK - 1][z]
+
+        phi(1, lambda z: errors[z], finish, reach=0, **near)
+
+    for i in range(len(pieces)):
+        near_copy(i).wait_send()
+        for k in range(1, pairs):
+            far_copy(i, k).wait_send()
+            pass_copy(i, k).wait_send()
+    for k in range(1, times):
+        @pl.when(t + k < times)
+        def _():
+            hop_copy(k).wait_send()
+    for j in range(times - 1):
+        @pl.when(t > j)
+        def _():
+            swap_copy(j).wait_send()
+
+
+def shallow_local(forcing, start_field, velocity, diffusivity):
+    spaces, times = lax.axis_size("space"), lax.axis_size("tm")
+    slab = forcing.shape[1]
+    plane = forcing.shape[2:]
+    depth, pad = spaces * slab, (BLOCK - 1) * SWEEPS
+    dma = pltpu.SemaphoreType.DMA
+    vmem = lambda *shape: pltpu.VMEM(shape + plane, jnp.float32)
+    padded = depth + 2 * pad
+    pieces, pairs = 4, max(spaces // 2 - 1, 1)
+    hbm = pl.BlockSpec(memory_space=pltpu.HBM)
+    return pl.pallas_call(
+        functools.partial(kernel, spaces, times),
+        out_shape=pltpu.VMEM(forcing.shape, forcing.dtype),
+        in_specs=[hbm] * 3 + [pl.BlockSpec(memory_space=pltpu.SMEM)],
+        out_specs=pl.BlockSpec(memory_space=pltpu.VMEM),
+        scratch_shapes=[
+            vmem(spaces, BLOCK + 4, slab), vmem(2, 6, padded), vmem(padded), vmem(padded),
+            vmem(padded), vmem(BLOCK, padded), vmem(times, depth), vmem(times, depth),
+            vmem(padded), vmem(2, padded),
+            dma((3,)), dma((pieces,)), dma((pieces,)),
+            dma((pairs, pieces)), dma((pairs, pieces)), dma((pairs, pieces)), dma((pairs, pieces)),
+            dma((times,)), dma((times,)), dma((times,)), dma((times,)),
+            pltpu.SemaphoreType.REGULAR((max(times, 3),)),
+        ],
+        compiler_params=pltpu.CompilerParams(
+            collective_id=0, has_side_effects=True),
+    )(forcing, start_field, velocity, diffusivity)
+
+
 def solution(mesh):
     placed = (
         P(("grp", "tm"), "space", None, None),
@@ -114,8 +459,9 @@
         P(None, "space", None, None),
         P("grp"),
     )
+    one_level = mesh.shape["tm"] == BLOCK and mesh.shape["space"] % 2 == 0
     return jax.shard_map(
-        local,
+        shallow_local if one_level else deep_local,
         mesh=mesh,
         in_specs=placed,
         out_specs=P(("grp", "tm"), "space", None, None),

time: 87.2 us -> 27 us (0.31)
  the two profiles are of different devices: /device:TPU:16 before, /device:TPU:25 now
where the time goes in v2:
time: 27 us; the launch traced here: 26.8 us
  Pallas kernels  25.5 us (94%)
  local copies, waits for them, and re-layouts  0.66 us (2%)
  between operations  0.66 us (2%)
    pallas_call x1, Pallas kernels, shallow_local(): pl.pallas_call(functools.partial(kernel, spaces, times), out_shape=pltpu....  25.5 us
    unnamed x1, local copies, waits for them, and re-layouts  0.66 us

profile of v2, /device:TPU:25, one launch (start us, length us, event | category | flops | bytes accessed | tf_op | source)
XLA Modules:
  0.0 26.8 jit_solution(13072260736710724470)
XLA Ops:
  0.7 25.5 %shard_map.46 = f32[4,8,8,128]{3,2,1,0:T(8,128)S(1)} custom-call(f32[4,8,8,128]{3,2,1,0:T(8,128)} %f_ref.1, f32[8,8,128]{2,1,0:T(8,128)} %u_ref.1, f32[3,8,8,128]{3,2,1,0:T(8,128)} %v_ref.1, f32[1]{0:T(128)S(6)} %copy.7.k_ref), custom_call_target="tpu_custom_call" | custom-call | tf_op jit(solution)/shard_map/pallas_call | solution.py:436
  26.2 0.7 %copy.6 = f32[4,8,8,128]{3,2,1,0:T(8,128)} copy(f32[4,8,8,128]{3,2,1,0:T(8,128)S(1)} %shard_map.46) | data formatting | bytes 262144
